TPU v7x, 256 devices: a whole 4x4x8 slice. The times are simulated.
256 devices in a mesh: shard: 64 (over z, y, core), model: 4 (over x).
Axes of the slice: x: 4, y: 4, z: 8, core: 2. Of those that a mesh axis runs over, the one named last changes fastest.
Arguments:
- gradients: float32 [256, 128, 4096], P(None, 'shard', 'model'), may hold values from -6 to 6
- momentum: float32 [256, 128, 4096], P(None, 'shard', 'model'), may hold values from -6 to 6
- weights: float32 [256, 128, 4096], P(None, 'shard', 'model'), may hold values from -0.1875 to 0.1875
Outputs:
- new_weights: float32 [256, 128, 4096], P(None, 'shard', 'model')
- new_momentum: float32 [256, 128, 4096], P(None, 'shard', 'model')
All inputs are finite; a program needn't handle non-finite values.
Results may differ from a plain program's by a relative error of at most 0.00015.
Values sent between devices are 32-bit elements; how exact they have to be, the bound alone decides.
A program may use at most 128 MiB of HBM per device.

v0:
```python
import jax
import jax.numpy as jnp
from jax import lax
from jax.sharding import PartitionSpec as P

ITERS = 4


hold_rate = 0.8
learn_rate = 1.0


def on_device(gradients, momentum, weights):
    new_momentum = hold_rate * momentum + gradients
    moved = lax.all_to_all(new_momentum, "shard", split_axis=0, concat_axis=1, tiled=True)
    whole = lax.all_to_all(moved, "model", split_axis=0, concat_axis=2, tiled=True)
    iterate = whole * lax.rsqrt(jnp.sum(whole * whole, axis=(1, 2), keepdims=True) + 1e-06)
    for step in range(ITERS):
        gram = jnp.einsum("mik,mjk->mij", iterate, iterate, precision=lax.Precision.HIGHEST)
        mixed = -4.775 * gram + 2.0315 * jnp.einsum(
            "mij,mjk->mik", gram, gram, precision=lax.Precision.HIGHEST
        )
        iterate = 3.4445 * iterate + jnp.einsum(
            "mij,mjk->mik", mixed, iterate, precision=lax.Precision.HIGHEST
        )
    iterate = lax.all_to_all(iterate, "model", split_axis=2, concat_axis=0, tiled=True)
    back = lax.all_to_all(iterate, "shard", split_axis=1, concat_axis=0, tiled=True)
    new_weights = weights - learn_rate * back
    return (new_weights, new_momentum)


def solution(mesh):
    placed = (P(None, "shard", "model"), P(None, "shard", "model"), P(None, "shard", "model"))
    return jax.shard_map(
        on_device,
        mesh=mesh,
        in_specs=placed,
        out_specs=(P(None, "shard", "model"), P(None, "shard", "model")),
        check_vma=False,
    )
```

profile of v0, /device:TPU:1, one launch (start us, length us, event | category | flops | bytes accessed | tf_op | source)
XLA Modules:
  0.0 227.7 jit_solution(10025155144655210961)
XLA Ops:
  0.6 3.7 %multiply_add_fusion = f32[256,2,1024]{2,1,0:T(2,128)S(1)} fusion(f32[256,2,1024]{2,1,0:T(2,128)} %param.3, f32[256,2,1024]{2,1,0:T(2,128)} %param.4), kind=kLoop, calls=%fused_computation.11 | loop fusion | flops 1048576 | bytes 6291456 | tf_op jit(solution)/shard_map/add | solution.py:14
  4.3 0.0 copy-start
  4.3 62.6 %all_to_all.63 = f32[256,2,1024]{2,1,0:T(2,128)S(1)} all-to-all(f32[256,2,1024]{2,1,0:T(2,128)S(1)} %multiply_add_fusion), channel_id=1, replica_groups=mesh['shard'=64,'model'=4] {'shard'}, dimensions={0} | all-to-all | bytes 4194304 | tf_op jit(solution)/shard_map/all_to_all | solution.py:15
  67.0 0.0 copy-done
  67.0 0.8 copy.32
  67.8 2.4 %all_to_all.49 = f32[4,128,1024]{2,1,0:T(8,128)} reshape(f32[4,64,2,1024]{3,2,1,0:T(2,128)S(1)} %bitcast.56) | data formatting | bytes 4194304 | tf_op jit(solution)/shard_map/all_to_all | solution.py:15
  70.2 28.1 %all_to_all.64 = f32[4,128,1024]{2,1,0:T(8,128)S(1)} all-to-all(f32[4,128,1024]{2,1,0:T(8,128)} %all_to_all.49), channel_id=1, replica_groups=mesh['shard'=64,'model'=4] {'model'}, dimensions={0} | all-to-all | bytes 4194304 | tf_op jit(solution)/shard_map/all_to_all | solution.py:16
  98.3 1.1 multiply_reduce_fusion
  100.1 1.8 fusion.4
  101.9 0.2 fusion.10
  102.1 2.6 %multiply_bitcast_fusion.1 = (f32[1,128,4,1024]{3,1,2,0:T(8,128)}, f32[1,128,4,1024]{3,1,2,0:T(8,128)}) fusion(f32[4,128,1024]{2,1,0:T(8,128)S(1)} %all_to_all.64, f32[]{:T(128)S(6)} %rsqrt.4), kind=kLoop, calls=%fused_computation.13 | loop fusion | flops 1048576 | bytes 6291460 | tf_op jit(solution)/shard_map/mul | solution.py:17
  104.7 1.9 copy.26
  106.6 2.9 %copy.25 = f32[1,128,4,1024]{1,3,2,0:T(8,128)} copy(f32[1,128,4,1024]{3,1,2,0:T(8,128)} %get-tuple-element.3) | data formatting | bytes 4194304 | tf_op jit(solution)/shard_map/mul | solution.py:23
  109.5 3.0 %copy.27 = f32[128,4096]{1,0:T(8,128)} copy(f32[128,4096]{0,1:T(8,128)} %bitcast.57) | data formatting | bytes 4194304 | tf_op jit(solution)/shard_map/mul | solution.py:23
  112.4 3.6 %convolution_add_fusion.3 = f32[128,4096]{1,0:T(8,128)S(1)} fusion(f32[128,4096]{1,0:T(8,128)} %copy.27, f32[128,128]{1,0:T(8,128)S(1)} %fusion.10, f32[128,4096]{0,1:T(8,128)S(1)} %bitcast.55), kind=kOutput, calls=%fused_computation.4 | convolution fusion | flops 805830656 | bytes 6356992 | tf_op jit(solution)/shard_map/mij,mjk->mik/dot_general | solution.py:23
  116.0 1.8 fusion.12
  117.8 0.2 fusion.9
  118.0 2.0 convolution_add_fusion.2
  120.1 1.8 fusion.13
  121.9 0.2 fusion.8
  122.1 2.0 convolution_add_fusion.1
  124.1 1.8 fusion.14
  125.9 0.2 fusion.7
  126.2 2.3 %fusion = f32[1,128,4096]{2,1,0:T(8,128)S(1)} fusion(f32[128,128]{1,0:T(8,128)S(1)} %fusion.7, f32[128,4096]{1,0:T(8,128)S(1)} %convolution_add_fusion.1), kind=kOutput, calls=%fused_computation.1 | convolution fusion | flops 806354944 | bytes 4259840 | tf_op jit(solution)/shard_map/mij,mjk->mik/dot_general | solution.py:23
  128.4 3.7 %copy.28 = f32[1,128,4096]{1,0,2:T(1,128)} copy(f32[1,128,4096]{2,1,0:T(8,128)S(1)} %fusion) | data formatting | bytes 4194304 | tf_op jit(solution)/shard_map/add | solution.py:23
  132.1 26.8 %all_to_all.65 = f32[1,128,4096]{1,0,2:T(1,128)S(1)} all-to-all(f32[1,128,4096]{1,0,2:T(1,128)} %copy.28), channel_id=1, replica_groups=mesh['shard'=64,'model'=4] {'model'}, dimensions={2} | all-to-all | bytes 4194304 | tf_op jit(solution)/shard_map/all_to_all | solution.py:26
  158.9 2.0 copy.29
  160.9 62.3 %all_to_all.66 = f32[4,128,1024]{2,0,1:T(4,128)S(1)} all-to-all(f32[4,128,1024]{2,0,1:T(4,128)} %bitcast.59), channel_id=1, replica_groups=mesh['shard'=64,'model'=4] {'shard'}, dimensions={1} | all-to-all | bytes 4194304 | tf_op jit(solution)/shard_map/all_to_all | solution.py:27
  223.2 0.0 copy-start.1
  223.2 1.9 copy.30
  225.1 0.0 copy-done.1
  225.1 2.5 %bitcast_subtract_fusion = f32[256,2,1024]{2,1,0:T(2,128)} fusion(f32[256,2,1024]{2,1,0:T(2,128)S(1)} %copy-done.1, f32[64,4,2,1024]{3,2,1,0:T(2,128)S(1)} %copy.30), kind=kLoop, calls=%fused_computation.7 | loop fusion | flops 524288 | bytes 6291456 | tf_op jit(solution)/shard_map/sub | solution.py:28
Async XLA Ops:
  4.3 62.7 %copy-start = (f32[256,2,1024]{2,1,0:T(2,128)}, f32[256,2,1024]{2,1,0:T(2,128)S(1)}, u32[]{:S(2)}) copy-start(f32[256,2,1024]{2,1,0:T(2,128)S(1)} %multiply_add_fusion) | copy-start | bytes 6291460
  223.2 1.9 copy-start.1
where the time goes:
time: 229 us; the launch traced here: 228 us
  blocking collectives  180 us (79%)
  local copies, waits for them, and re-layouts  18.6 us (8%)
  matrix products  17.9 us (8%)
  other arithmetic  9.89 us (4%)
    all_to_all x1, blocking collectives, on_device(): lax.all_to_all(new_momentum, 'shard', split_axis=0, concat_axis=1, tiled=...  62.6 us
    all_to_all x1, blocking collectives, on_device(): lax.all_to_all(iterate, 'shard', split_axis=1, concat_axis=0, tiled=True)  62.3 us
    all_to_all x1, blocking collectives, on_device(): lax.all_to_all(moved, 'model', split_axis=0, concat_axis=2, tiled=True)  28.1 us
    all_to_all x1, blocking collectives, on_device(): lax.all_to_all(iterate, 'model', split_axis=2, concat_axis=0, tiled=True)  26.8 us
    dot_general x4, matrix products, on_device(): jnp.einsum('mij,mjk->mik', mixed, iterate, precision=lax.Precision.HIGHEST)  9.94 us
    dot_general x4, matrix products, on_device(): jnp.einsum('mik,mjk->mij', iterate, iterate, precision=lax.Precision.HIGH...  7.16 us
    mul x2, local copies, waits for them, and re-layouts, on_device(): 3.4445 * iterate  5.84 us

commit v1 on v0

v1 whole, which is shorter than its diff:
```python
import functools

import jax
import jax.numpy as jnp
from jax import lax
from jax.experimental import pallas as pl
from jax.experimental.pallas import tpu as pltpu
from jax.sharding import PartitionSpec as P

ITERS = 4
hold_rate = 0.8
learn_rate = 1.0

GROUPS = 64
COLUMNS = 4
OWNED = 4
SIDE = 128
LANES = 128
TILES = 8
PIECE = 16
DZ_ORDER = (4, 3, 5, 2, 6, 1, 7, 0)
HIGH = lax.Precision.HIGHEST


def dot(a, b, ca, cb):
    return lax.dot_general(
        a, b, (((ca,), (cb,)), ((), ())), precision=HIGH, preferred_element_type=jnp.float32
    )


def peer_of(me, dz, k):
    z, y, core = me // 8, (me // 2) % 4, me % 2
    return ((z + dz) % 8) * 8 + ((y + k // 2) % 4) * 2 + (core + k % 2) % 2


def kernel(moved_ref, back_ref, land, res, parts, f_send, f_recv, g_send, g_recv, b_send, b_recv):
    me = lax.axis_index("shard")
    col = lax.axis_index("model")

    def at(peer):
        return (peer, col)

    barrier = pltpu.get_barrier_semaphore()

    def greet(k, _):
        pl.semaphore_signal(barrier, inc=1, device_id=at((me + k) % GROUPS), device_id_type=pl.DeviceIdType.MESH)
        return 0

    lax.fori_loop(1, GROUPS, greet, 0)
    for d in range(1, COLUMNS):
        pl.semaphore_signal(
            barrier, inc=1, device_id=(me, (col + d) % COLUMNS), device_id_type=pl.DeviceIdType.MESH
        )
    pl.semaphore_wait(barrier, GROUPS - 1 + COLUMNS - 1)

    mine = pl.multiple_of(me * PIECE, PIECE)

    def send_rows(m):
        for dz in DZ_ORDER:
            def one(k, _, dz=dz):
                peer = peer_of(me, dz, k)
                pltpu.make_async_remote_copy(
                    src_ref=moved_ref.at[peer * OWNED + m],
                    dst_ref=land.at[m, pl.ds(mine, PIECE), :],
                    send_sem=f_send.at[m],
                    recv_sem=f_recv.at[m],
                    device_id=at(peer),
                    device_id_type=pl.DeviceIdType.MESH,
                ).start()
                return 0
            lax.fori_loop(1 if dz == 0 else 0, 8, one, 0)

    for m in range(OWNED):
        send_rows(m)
    for m in range(OWNED):
        land[m, pl.ds(mine, PIECE), :] = moved_ref[me * OWNED + m]

    def tile_pair(m, j):
        sides = []
        for q in (2 * j, 2 * j + 1):
            sides.append(
                jnp.concatenate(
                    [land[m, pl.ds(2 * q + r, GROUPS, stride=PIECE), :] for r in (0, 1)], axis=0
                )
            )
        return jnp.concatenate(sides, axis=1)

    def wait_bytes(ref, sem):
        pltpu.make_async_copy(ref, ref, sem).wait()

    rows = lax.broadcasted_iota(jnp.int32, (SIDE, SIDE), 0)
    cols = lax.broadcasted_iota(jnp.int32, (SIDE, SIDE), 1)
    eye = jnp.where(rows == cols, 1.0, 0.0).astype(jnp.float32)

    def gram(m):
        wait_bytes(land.at[m, pl.ds(0, (GROUPS - 1) * PIECE), :], f_recv.at[m])
        total = None
        for j in range(TILES // 2):
            x = tile_pair(m, j)
            term = dot(x, x, 1, 1)
            total = term if total is None else total + term
        parts[m, col] = total
        for d in range(1, COLUMNS):
            pltpu.make_async_remote_copy(
                src_ref=parts.at[m, col],
                dst_ref=parts.at[m, col],
                send_sem=g_send.at[m],
                recv_sem=g_recv.at[m],
                device_id=(me, (col + d) % COLUMNS),
                device_id_type=pl.DeviceIdType.MESH,
            ).start()

    def finish(m):
        wait_bytes(parts.at[m, pl.ds(0, COLUMNS - 1)], g_recv.at[m])
        whole = (parts[m, 0] + parts[m, 1]) + (parts[m, 2] + parts[m, 3])
        power = jnp.sum(jnp.sum(whole * eye, axis=1, keepdims=True), axis=0, keepdims=True)
        scale = lax.rsqrt(power + 1e-06)
        a = whole * (scale * scale)
        product = None
        for step in range(ITERS):
            mixed = 3.4445 * eye - 4.775 * a + 2.0315 * dot(a, a, 1, 0)
            product = mixed if product is None else dot(mixed, product, 1, 0)
            if step < ITERS - 1:
                a = dot(dot(mixed, a, 1, 0), mixed, 1, 0)
        product = product * scale
        for j in range(TILES // 2):
            y = dot(product, tile_pair(m, j), 1, 0)
            for i in (0, 1):
                q = 2 * j + i
                for r in (0, 1):
                    res[m, pl.ds(2 * q + r, GROUPS, stride=PIECE), :] = y[
                        GROUPS * r : GROUPS * (r + 1), LANES * i : LANES * (i + 1)
                    ]
        for dz in DZ_ORDER:
            def one(k, _, dz=dz):
                peer = peer_of(me, dz, k)
                pltpu.make_async_remote_copy(
                    src_ref=res.at[m, pl.ds(pl.multiple_of(peer * PIECE, PIECE), PIECE), :],
                    dst_ref=back_ref.at[me * OWNED + m],
                    send_sem=b_send.at[m],
                    recv_sem=b_recv,
                    device_id=at(peer),
                    device_id_type=pl.DeviceIdType.MESH,
                ).start()
                return 0
            lax.fori_loop(1 if dz == 0 else 0, 8, one, 0)
        back_ref[me * OWNED + m] = res[m, pl.ds(mine, PIECE), :]

    gram(0)
    for m in range(OWNED):
        if m + 1 < OWNED:
            pass
        finish(m)
        if m + 1 < OWNED:
            gram(m + 1)

    for m in range(OWNED):
        wait_bytes(land.at[m, pl.ds(0, (GROUPS - 1) * PIECE), :], f_send.at[m])
        wait_bytes(parts.at[m, pl.ds(0, COLUMNS - 1)], g_send.at[m])
        wait_bytes(res.at[m, pl.ds(0, (GROUPS - 1) * PIECE), :], b_send.at[m])
    wait_bytes(back_ref.at[pl.ds(0, (GROUPS - 1) * OWNED)], b_recv)


def exchange(pieces):
    return pl.pallas_call(
        kernel,
        out_shape=jax.ShapeDtypeStruct(pieces.shape, jnp.float32),
        in_specs=[pl.BlockSpec(memory_space=pltpu.VMEM)],
        out_specs=pl.BlockSpec(memory_space=pltpu.VMEM),
        scratch_shapes=[
            pltpu.VMEM((OWNED, GROUPS * PIECE, LANES), jnp.float32),
            pltpu.VMEM((OWNED, GROUPS * PIECE, LANES), jnp.float32),
            pltpu.VMEM((OWNED, COLUMNS, SIDE, SIDE), jnp.float32),
            pltpu.SemaphoreType.DMA((OWNED,)),
            pltpu.SemaphoreType.DMA((OWNED,)),
            pltpu.SemaphoreType.DMA((OWNED,)),
            pltpu.SemaphoreType.DMA((OWNED,)),
            pltpu.SemaphoreType.DMA((OWNED,)),
            pltpu.SemaphoreType.DMA,
        ],
        compiler_params=pltpu.CompilerParams(
            collective_id=0, has_side_effects=True, vmem_limit_bytes=24 * 1024 * 1024
        ),
    )(pieces)


def to_pieces(block):
    mats = block.shape[0]
    return block.reshape(mats, 2, TILES, LANES).transpose(0, 2, 1, 3).reshape(mats, PIECE, LANES)


def from_pieces(pieces):
    mats = pieces.shape[0]
    return pieces.reshape(mats, TILES, 2, LANES).transpose(0, 2, 1, 3).reshape(mats, 2, TILES * LANES)


def on_device(gradients, momentum, weights):
    new_momentum = hold_rate * momentum + gradients
    back = from_pieces(exchange(to_pieces(new_momentum)))
    new_weights = weights - learn_rate * back
    return (new_weights, new_momentum)


def solution(mesh):
    placed = (P(None, "shard", "model"), P(None, "shard", "model"), P(None, "shard", "model"))
    return jax.shard_map(
        on_device,
        mesh=mesh,
        in_specs=placed,
        out_specs=(P(None, "shard", "model"), P(None, "shard", "model")),
        check_vma=False,
    )
```

time: 229 us -> 111 us (0.48)
  blocking collectives: 180 us -> 0 us
  Pallas kernels: 0 us -> 104 us
  local copies, waits for them, and re-layouts: 18.6 us -> 0.01 us
  matrix products: 17.9 us -> 0 us
  other arithmetic: 9.89 us -> 6.06 us
    all_to_all x4 -> x0, blocking collectives: 180 us -> none  [the longest x1 62.6 us: on_device(): lax.all_to_all(new_momentum, 'shard', split_axis=0, concat_axis=1, tiled=...]
    pallas_call x0 -> x1, Pallas kernels: none -> 104 us  [exchange(): pl.pallas_call(kernel, out_shape=jax.ShapeDtypeStruct(pieces.shape, jnp.f...]
    dot_general x12 -> x0, matrix products: 17.9 us -> none  [the longest x4 9.94 us: on_device(): jnp.einsum('mij,mjk->mik', mixed, iterate, precision=lax.Precision.HIGHEST)]
    mul x3 -> x0, local copies, waits for them, and re-layouts: 7.74 us -> none  [the longest x2 5.84 us: on_device(): 3.4445 * iterate]
    all_to_all x4 -> x0, local copies, waits for them, and re-layouts: 7.13 us -> none  [the longest x2 3.24 us: on_device(): lax.all_to_all(new_momentum, 'shard', split_axis=0, concat_axis=1, tiled=...]
    add x1 -> x0, local copies, waits for them, and re-layouts: 3.7 us -> none  [on_device(): 3.4445 * iterate]
    mul x1 -> x0, other arithmetic: 2.56 us -> none  [on_device(): whole * lax.rsqrt(jnp.sum(whole * whole, axis=(1, 2), keepdims=True) + 1e...]
where the time goes in v1:
time: 111 us
  Pallas kernels  104 us (94%)
  other arithmetic  6.06 us (5%)
    pallas_call x1, Pallas kernels, exchange(): pl.pallas_call(kernel, out_shape=jax.ShapeDtypeStruct(pieces.shape, jnp.f...  104 us
    add x1, other arithmetic, on_device(): new_momentum = hold_rate * momentum + gradients  3.66 us
    sub x1, other arithmetic, on_device(): new_weights = weights - learn_rate * back  2.4 us

profile of v1, /device:TPU:1, one launch (start us, length us, event | category | flops | bytes accessed | tf_op | source)
XLA Modules:
  0.0 111.0 jit_solution(12646266231013038678)
XLA Ops:
  0.6 3.7 %multiply_add_fusion = f32[256,2,1024]{2,1,0:T(2,128)S(1)} fusion(f32[256,2,1024]{2,1,0:T(2,128)} %param.3, f32[256,2,1024]{2,1,0:T(2,128)} %param.4), kind=kLoop, calls=%fused_computation | loop fusion | flops 1048576 | bytes 6291456 | tf_op jit(solution)/shard_map/add | solution.py:198
  4.3 0.0 copy-start
  4.3 0.0 copy-start.1
  4.3 104.3 %shard_map.50 = f32[256,16,128]{2,1,0:T(8,128)S(1)} custom-call(f32[256,16,128]{2,1,0:T(8,128)S(1)} %bitcast.10), custom_call_target="tpu_custom_call" | custom-call | tf_op jit(solution)/shard_map/pallas_call | solution.py:165
  108.6 0.0 copy-done
  108.6 0.0 copy-done.1
  108.6 2.4 %sub.3 = f32[256,2,1024]{2,1,0:T(2,128)} subtract(f32[256,2,1024]{2,1,0:T(2,128)S(1)} %copy-done.1, f32[256,2,1024]{2,1,0:T(2,128)S(1)} %bitcast.11) | non-fusion elementwise | flops 524288 | bytes 6291456 | tf_op jit(solution)/shard_map/sub | solution.py:200
Async XLA Ops:
  4.3 104.3 %copy-start = (f32[256,2,1024]{2,1,0:T(2,128)}, f32[256,2,1024]{2,1,0:T(2,128)S(1)}, u32[]{:S(2)}) copy-start(f32[256,2,1024]{2,1,0:T(2,128)S(1)} %multiply_add_fusion) | copy-start | bytes 6291460
  4.3 104.3 %copy-start.1 = (f32[256,2,1024]{2,1,0:T(2,128)S(1)}, f32[256,2,1024]{2,1,0:T(2,128)}, u32[]{:S(2)}) copy-start(f32[256,2,1024]{2,1,0:T(2,128)} %param.5) | copy-start | bytes 6291460

commit v2 on v1

--- a/solution.py
+++ b/solution.py
@@ -19,6 +19,8 @@
 TILES = 8
 PIECE = 16
 DZ_ORDER = (4, 3, 5, 2, 6, 1, 7, 0)
+NEAR = [(dz, k) for dz in DZ_ORDER[:-1] for k in (0, 1)] + [(0, k) for k in (4, 5, 2, 3, 6, 7, 1)]
+EARLY = 2
 HIGH = lax.Precision.HIGHEST
 
 
@@ -33,47 +35,81 @@
     return ((z + dz) % 8) * 8 + ((y + k // 2) % 4) * 2 + (core + k % 2) % 2
 
 
-def kernel(moved_ref, back_ref, land, res, parts, f_send, f_recv, g_send, g_recv, b_send, b_recv):
+def kernel(
+    grad_ref, mom_ref, weight_ref, new_weight_ref, moved_ref,
+    grad, mom, weight, land, res, parts, back,
+    ready, in_sem, w_sem, f_send, f_recv, g_send, g_recv, b_send, b_recv,
+):
     me = lax.axis_index("shard")
     col = lax.axis_index("model")
 
     def at(peer):
         return (peer, col)
 
+    z = me // 8
+    loads = []
+    for i, dz in enumerate(DZ_ORDER):
+        block = pl.ds(((z + dz) % 8) * 8, 8)
+        for j, (ref, buf) in enumerate(((grad_ref, grad), (mom_ref, mom))):
+            copy = pltpu.make_async_copy(ref.at[block], buf.at[block], in_sem.at[2 * i + j])
+            copy.start()
+            loads.append(copy)
+
     barrier = pltpu.get_barrier_semaphore()
-
-    def greet(k, _):
-        pl.semaphore_signal(barrier, inc=1, device_id=at((me + k) % GROUPS), device_id_type=pl.DeviceIdType.MESH)
-        return 0
-
-    lax.fori_loop(1, GROUPS, greet, 0)
+    for dz, k in NEAR:
+        pl.semaphore_signal(
+            barrier, inc=1, device_id=at(peer_of(me, dz, k)), device_id_type=pl.DeviceIdType.MESH
+        )
     for d in range(1, COLUMNS):
         pl.semaphore_signal(
             barrier, inc=1, device_id=(me, (col + d) % COLUMNS), device_id_type=pl.DeviceIdType.MESH
         )
-    pl.semaphore_wait(barrier, GROUPS - 1 + COLUMNS - 1)
+
+    load_weight = pltpu.make_async_copy(weight_ref, weight, w_sem)
+    load_weight.start()
 
     mine = pl.multiple_of(me * PIECE, PIECE)
 
-    def send_rows(m):
+    def send_row(m, dz, k):
+        peer = peer_of(me, dz, k)
+        pltpu.make_async_remote_copy(
+            src_ref=moved_ref.at[peer, m],
+            dst_ref=land.at[m, pl.ds(mine, PIECE), :],
+            send_sem=f_send.at[m],
+            recv_sem=f_recv.at[m],
+            device_id=at(peer),
+            device_id_type=pl.DeviceIdType.MESH,
+        ).start()
+
+    def send_rows(m, dz, low):
+        def one(k, _):
+            send_row(m, dz, k)
+            return 0
+
+        lax.fori_loop(low, 8, one, 0)
+
+    for i, dz in enumerate(DZ_ORDER):
+        block = pl.ds(((z + dz) % 8) * 8, 8)
+        loads[2 * i].wait()
+        loads[2 * i + 1].wait()
+        moved_ref[block] = hold_rate * mom[block] + grad[block]
+        if i == 0:
+            pl.semaphore_wait(barrier, len(NEAR) + COLUMNS - 1)
+            for far in DZ_ORDER[:-1]:
+                pl.semaphore_signal(
+                    ready, inc=1, device_id=at(peer_of(me, far, 0)), device_id_type=pl.DeviceIdType.MESH
+                )
+        if dz:
+            for m in range(EARLY):
+                for k in (0, 1):
+                    send_row(m, dz, k)
+
+    pl.semaphore_wait(ready, len(DZ_ORDER) - 1)
+    for m in range(OWNED):
         for dz in DZ_ORDER:
-            def one(k, _, dz=dz):
-                peer = peer_of(me, dz, k)
-                pltpu.make_async_remote_copy(
-                    src_ref=moved_ref.at[peer * OWNED + m],
-                    dst_ref=land.at[m, pl.ds(mine, PIECE), :],
-                    send_sem=f_send.at[m],
-                    recv_sem=f_recv.at[m],
-                    device_id=at(peer),
-                    device_id_type=pl.DeviceIdType.MESH,
-                ).start()
-                return 0
-            lax.fori_loop(1 if dz == 0 else 0, 8, one, 0)
-
-    for m in range(OWNED):
-        send_rows(m)
-    for m in range(OWNED):
-        land[m, pl.ds(mine, PIECE), :] = moved_ref[me * OWNED + m]
+            send_rows(m, dz, 1 if dz == 0 else 2 if m < EARLY else 0)
+    for m in range(OWNED):
+        land[m, pl.ds(mine, PIECE), :] = moved_ref[me, m]
 
     def tile_pair(m, j):
         sides = []
@@ -136,15 +172,15 @@
                 peer = peer_of(me, dz, k)
                 pltpu.make_async_remote_copy(
                     src_ref=res.at[m, pl.ds(pl.multiple_of(peer * PIECE, PIECE), PIECE), :],
-                    dst_ref=back_ref.at[me * OWNED + m],
+                    dst_ref=back.at[me, m],
                     send_sem=b_send.at[m],
-                    recv_sem=b_recv,
+                    recv_sem=b_recv.at[m],
                     device_id=at(peer),
                     device_id_type=pl.DeviceIdType.MESH,
                 ).start()
                 return 0
             lax.fori_loop(1 if dz == 0 else 0, 8, one, 0)
-        back_ref[me * OWNED + m] = res[m, pl.ds(mine, PIECE), :]
+        back[me, m] = res[m, pl.ds(mine, PIECE), :]
 
     gram(0)
     for m in range(OWNED):
@@ -154,51 +190,85 @@
         if m + 1 < OWNED:
             gram(m + 1)
 
+    load_weight.wait()
+    for m in range(OWNED):
+        wait_bytes(back.at[pl.ds(0, GROUPS - 1), m], b_recv.at[m])
+        new_weight_ref[:, m] = weight[:, m] - learn_rate * back[:, m]
+
     for m in range(OWNED):
         wait_bytes(land.at[m, pl.ds(0, (GROUPS - 1) * PIECE), :], f_send.at[m])
         wait_bytes(parts.at[m, pl.ds(0, COLUMNS - 1)], g_send.at[m])
         wait_bytes(res.at[m, pl.ds(0, (GROUPS - 1) * PIECE), :], b_send.at[m])
-    wait_bytes(back_ref.at[pl.ds(0, (GROUPS - 1) * OWNED)], b_recv)
-
-
-def exchange(pieces):
+
+
+def update(gradients, momentum, weights):
+    whole = pltpu.VMEM(gradients.shape, jnp.float32)
     return pl.pallas_call(
         kernel,
-        out_shape=jax.ShapeDtypeStruct(pieces.shape, jnp.float32),
-        in_specs=[pl.BlockSpec(memory_space=pltpu.VMEM)],
-        out_specs=pl.BlockSpec(memory_space=pltpu.VMEM),
+        out_shape=[jax.ShapeDtypeStruct(gradients.shape, jnp.float32)] * 2,
+        in_specs=[pl.BlockSpec(memory_space=pltpu.HBM)] * 3,
+        out_specs=[pl.BlockSpec(memory_space=pltpu.VMEM)] * 2,
         scratch_shapes=[
+            whole,
+            whole,
+            whole,
             pltpu.VMEM((OWNED, GROUPS * PIECE, LANES), jnp.float32),
             pltpu.VMEM((OWNED, GROUPS * PIECE, LANES), jnp.float32),
             pltpu.VMEM((OWNED, COLUMNS, SIDE, SIDE), jnp.float32),
-            pltpu.SemaphoreType.DMA((OWNED,)),
-            pltpu.SemaphoreType.DMA((OWNED,)),
-            pltpu.SemaphoreType.DMA((OWNED,)),
-            pltpu.SemaphoreType.DMA((OWNED,)),
-            pltpu.SemaphoreType.DMA((OWNED,)),
+            whole,
+            pltpu.SemaphoreType.REGULAR,
+            pltpu.SemaphoreType.DMA((16,)),
             pltpu.SemaphoreType.DMA,
+            pltpu.SemaphoreType.DMA((OWNED,)),
+            pltpu.SemaphoreType.DMA((OWNED,)),
+            pltpu.SemaphoreType.DMA((OWNED,)),
+            pltpu.SemaphoreType.DMA((OWNED,)),
+            pltpu.SemaphoreType.DMA((OWNED,)),
+            pltpu.SemaphoreType.DMA((OWNED,)),
         ],
         compiler_params=pltpu.CompilerParams(
-            collective_id=0, has_side_effects=True, vmem_limit_bytes=24 * 1024 * 1024
+            collective_id=0, has_side_effects=True, vmem_limit_bytes=48 * 1024 * 1024
         ),
-    )(pieces)
+    )(gradients, momentum, weights)
+
+
+def store_kernel(new_weight_ref, moved_ref, weight_out, moved_out, sems):
+    copies = [
+        pltpu.make_async_copy(new_weight_ref, weight_out, sems.at[0]),
+        pltpu.make_async_copy(moved_ref, moved_out, sems.at[1]),
+    ]
+    for copy in copies:
+        copy.start()
+    for copy in copies:
+        copy.wait()
+
+
+def store(new_weights, new_momentum):
+    return pl.pallas_call(
+        store_kernel,
+        out_shape=[jax.ShapeDtypeStruct(new_weights.shape, jnp.float32)] * 2,
+        in_specs=[pl.BlockSpec(memory_space=pltpu.VMEM)] * 2,
+        out_specs=[pl.BlockSpec(memory_space=pltpu.HBM)] * 2,
+        scratch_shapes=[pltpu.SemaphoreType.DMA((2,))],
+        compiler_params=pltpu.CompilerParams(vmem_limit_bytes=1024 * 1024),
+    )(new_weights, new_momentum)
 
 
 def to_pieces(block):
-    mats = block.shape[0]
-    return block.reshape(mats, 2, TILES, LANES).transpose(0, 2, 1, 3).reshape(mats, PIECE, LANES)
+    block = block.reshape(GROUPS, OWNED, 2, TILES, LANES).transpose(0, 1, 3, 2, 4)
+    return block.reshape(GROUPS, OWNED, PIECE, LANES)
 
 
 def from_pieces(pieces):
-    mats = pieces.shape[0]
-    return pieces.reshape(mats, TILES, 2, LANES).transpose(0, 2, 1, 3).reshape(mats, 2, TILES * LANES)
+    pieces = pieces.reshape(GROUPS, OWNED, TILES, 2, LANES).transpose(0, 1, 3, 2, 4)
+    return pieces.reshape(GROUPS * OWNED, 2, TILES * LANES)
 
 
 def on_device(gradients, momentum, weights):
-    new_momentum = hold_rate * momentum + gradients
-    back = from_pieces(exchange(to_pieces(new_momentum)))
-    new_weights = weights - learn_rate * back
-    return (new_weights, new_momentum)
+    new_weights, new_momentum = store(
+        *update(to_pieces(gradients), to_pieces(momentum), to_pieces(weights))
+    )
+    return (from_pieces(new_weights), from_pieces(new_momentum))
 
 
 def solution(mesh):

time: 111 us -> 106 us (0.955)
  other arithmetic: 6.06 us -> 0 us
  Pallas kernels: 104 us -> 106 us
    add x1 -> x0, other arithmetic: 3.66 us -> none  [on_device(): new_momentum = hold_rate * momentum + gradients]
    sub x1 -> x0, other arithmetic: 2.4 us -> none  [on_device(): new_weights = weights - learn_rate * back]
    pallas_call x1 -> x2, Pallas kernels: 104 us -> 106 us  [the longest x1 104 us: update(): pl.pallas_call(kernel, out_shape=[jax.ShapeDtypeStruct(gradients.shape, j...]
where the time goes in v2:
time: 106 us
  Pallas kernels  106 us (100%)
    pallas_call x1, Pallas kernels, update(): pl.pallas_call(kernel, out_shape=[jax.ShapeDtypeStruct(gradients.shape, j...  104 us

profile of v2, /device:TPU:1, one launch (start us, length us, event | category | flops | bytes accessed | tf_op | source)
XLA Modules:
  0.0 106.3 jit_solution(1384341206354538958)
XLA Ops:
  0.6 103.6 %shard_map.50 = (f32[64,4,16,128]{3,2,1,0:T(8,128)S(1)}, f32[64,4,16,128]{3,2,1,0:T(8,128)S(1)}) custom-call(f32[64,4,16,128]{3,2,1,0:T(8,128)} %bitcast.25, f32[64,4,16,128]{3,2,1,0:T(8,128)} %bitcast.26, f32[64,4,16,128]{3,2,1,0:T(8,128)} %bitcast.27), custom_call_target="tpu_custom_call" | custom-call | tf_op jit(solution)/shard_map/pallas_call | solution.py:206
  104.2 2.0 %shard_map.51 = (f32[64,4,16,128]{3,2,1,0:T(8,128)}, f32[64,4,16,128]{3,2,1,0:T(8,128)}) custom-call(f32[64,4,16,128]{3,2,1,0:T(8,128)S(1)} %get-tuple-element.6.new_weight_ref, f32[64,4,16,128]{3,2,1,0:T(8,128)S(1)} %get-tuple-element.7.moved_ref), custom_call_target="tpu_custom_call" | custom-call | tf_op jit(solution)/shard_map/pallas_call | solution.py:247

commit v3 on v2

--- a/solution.py
+++ b/solution.py
@@ -21,6 +21,8 @@
 DZ_ORDER = (4, 3, 5, 2, 6, 1, 7, 0)
 NEAR = [(dz, k) for dz in DZ_ORDER[:-1] for k in (0, 1)] + [(0, k) for k in (4, 5, 2, 3, 6, 7, 1)]
 EARLY = 2
+BY_DISTANCE = 3
+Z_ORDER = ((0,), (1, 2), (3, 7), (4, 5, 6))
 HIGH = lax.Precision.HIGHEST
 
 
@@ -167,19 +169,36 @@
                     res[m, pl.ds(2 * q + r, GROUPS, stride=PIECE), :] = y[
                         GROUPS * r : GROUPS * (r + 1), LANES * i : LANES * (i + 1)
                     ]
-        for dz in DZ_ORDER:
-            def one(k, _, dz=dz):
-                peer = peer_of(me, dz, k)
-                pltpu.make_async_remote_copy(
-                    src_ref=res.at[m, pl.ds(pl.multiple_of(peer * PIECE, PIECE), PIECE), :],
-                    dst_ref=back.at[me, m],
-                    send_sem=b_send.at[m],
-                    recv_sem=b_recv.at[m],
-                    device_id=at(peer),
-                    device_id_type=pl.DeviceIdType.MESH,
-                ).start()
-                return 0
-            lax.fori_loop(1 if dz == 0 else 0, 8, one, 0)
+        def send_back(peer):
+            pltpu.make_async_remote_copy(
+                src_ref=res.at[m, pl.ds(pl.multiple_of(peer * PIECE, PIECE), PIECE), :],
+                dst_ref=back.at[me, m],
+                send_sem=b_send.at[m],
+                recv_sem=b_recv.at[m],
+                device_id=at(peer),
+                device_id_type=pl.DeviceIdType.MESH,
+            ).start()
+
+        if m < BY_DISTANCE:
+            for dz in DZ_ORDER:
+                def one(k, _, dz=dz):
+                    send_back(peer_of(me, dz, k))
+                    return 0
+
+                lax.fori_loop(1 if dz == 0 else 0, 8, one, 0)
+        else:
+            for heres in Z_ORDER:
+                def one(k, _, heres=heres):
+                    for there in heres:
+                        peer = there * 8 + k
+
+                        @pl.when(peer != me)
+                        def _():
+                            send_back(peer)
+
+                    return 0
+
+                lax.fori_loop(0, 8, one, 0)
         back[me, m] = res[m, pl.ds(mine, PIECE), :]
 
     gram(0)

time: 106 us -> 103 us (0.972)
  the two profiles are of different devices: /device:TPU:1 before, /device:TPU:57 now
where the time goes in v3:
time: 103 us
  Pallas kernels  102 us (99%)
    pallas_call x1, Pallas kernels, update(): pl.pallas_call(kernel, out_shape=[jax.ShapeDtypeStruct(gradients.shape, j...  100 us

profile of v3, /device:TPU:57, one launch (start us, length us, event | category | flops | bytes accessed | tf_op | source)
XLA Modules:
  0.0 103.0 jit_solution(17913360866314214859)
XLA Ops:
  0.6 100.4 %shard_map.50 = (f32[64,4,16,128]{3,2,1,0:T(8,128)S(1)}, f32[64,4,16,128]{3,2,1,0:T(8,128)S(1)}) custom-call(f32[64,4,16,128]{3,2,1,0:T(8,128)} %bitcast.25, f32[64,4,16,128]{3,2,1,0:T(8,128)} %bitcast.26, f32[64,4,16,128]{3,2,1,0:T(8,128)} %bitcast.27), custom_call_target="tpu_custom_call" | custom-call | tf_op jit(solution)/shard_map/pallas_call | solution.py:225
  101.0 2.0 %shard_map.51 = (f32[64,4,16,128]{3,2,1,0:T(8,128)}, f32[64,4,16,128]{3,2,1,0:T(8,128)}) custom-call(f32[64,4,16,128]{3,2,1,0:T(8,128)S(1)} %get-tuple-element.6.new_weight_ref, f32[64,4,16,128]{3,2,1,0:T(8,128)S(1)} %get-tuple-element.7.moved_ref), custom_call_target="tpu_custom_call" | custom-call | tf_op jit(solution)/shard_map/pallas_call | solution.py:266

commit v4 on v3

--- a/solution.py
+++ b/solution.py
@@ -19,10 +19,15 @@
 TILES = 8
 PIECE = 16
 DZ_ORDER = (4, 3, 5, 2, 6, 1, 7, 0)
-NEAR = [(dz, k) for dz in DZ_ORDER[:-1] for k in (0, 1)] + [(0, k) for k in (4, 5, 2, 3, 6, 7, 1)]
-EARLY = 2
+FIRST = (0, 1)
+NEAR = [(dz, k) for dz in (1, 7) for k in FIRST] + [(0, k) for k in (4, 5, 2, 3, 6, 7, 1)]
+LOAD_ORDER = (1, 7, 2, 6, 3, 5, 4, 0)
+W2 = 1
+W3 = 1
 BY_DISTANCE = 3
-Z_ORDER = ((0,), (1, 2), (3, 7), (4, 5, 6))
+Z_LATE = (0.0, 0.9, 1.9, 2.8, 3.9, 4.8, 4.8, 3.9)
+Y_LATE = (0.0, 0.8, 1.6, 1.8)
+CELLS = sorted(range(32), key=lambda cell: (1 * Z_LATE[cell // 4] + 2 * Y_LATE[cell % 4], cell))
 HIGH = lax.Precision.HIGHEST
 
 
@@ -39,7 +44,7 @@
 
 def kernel(
     grad_ref, mom_ref, weight_ref, new_weight_ref, moved_ref,
-    grad, mom, weight, land, res, parts, back,
+    grad, mom, weight, land, res, parts, back, mid,
     ready, in_sem, w_sem, f_send, f_recv, g_send, g_recv, b_send, b_recv,
 ):
     me = lax.axis_index("shard")
@@ -50,27 +55,40 @@
 
     z = me // 8
     loads = []
-    for i, dz in enumerate(DZ_ORDER):
+
+    def load(i, dz):
         block = pl.ds(((z + dz) % 8) * 8, 8)
         for j, (ref, buf) in enumerate(((grad_ref, grad), (mom_ref, mom))):
             copy = pltpu.make_async_copy(ref.at[block], buf.at[block], in_sem.at[2 * i + j])
             copy.start()
             loads.append(copy)
 
+    def signal(sem, dz, k):
+        pl.semaphore_signal(
+            sem, inc=1, device_id=at(peer_of(me, dz, k)), device_id_type=pl.DeviceIdType.MESH
+        )
+
+    load(0, LOAD_ORDER[0])
     barrier = pltpu.get_barrier_semaphore()
     for dz, k in NEAR:
-        pl.semaphore_signal(
-            barrier, inc=1, device_id=at(peer_of(me, dz, k)), device_id_type=pl.DeviceIdType.MESH
-        )
+        signal(barrier, dz, k)
     for d in range(1, COLUMNS):
         pl.semaphore_signal(
             barrier, inc=1, device_id=(me, (col + d) % COLUMNS), device_id_type=pl.DeviceIdType.MESH
         )
-
+    for i, dz in enumerate(LOAD_ORDER):
+        if i:
+            load(i, dz)
     load_weight = pltpu.make_async_copy(weight_ref, weight, w_sem)
     load_weight.start()
 
     mine = pl.multiple_of(me * PIECE, PIECE)
+
+    def momentum_of(i):
+        block = pl.ds(((z + LOAD_ORDER[i]) % 8) * 8, 8)
+        loads[2 * i].wait()
+        loads[2 * i + 1].wait()
+        moved_ref[block] = hold_rate * mom[block] + grad[block]
 
     def send_row(m, dz, k):
         peer = peer_of(me, dz, k)
@@ -90,26 +108,44 @@
 
         lax.fori_loop(low, 8, one, 0)
 
-    for i, dz in enumerate(DZ_ORDER):
-        block = pl.ds(((z + dz) % 8) * 8, 8)
-        loads[2 * i].wait()
-        loads[2 * i + 1].wait()
-        moved_ref[block] = hold_rate * mom[block] + grad[block]
-        if i == 0:
-            pl.semaphore_wait(barrier, len(NEAR) + COLUMNS - 1)
-            for far in DZ_ORDER[:-1]:
-                pl.semaphore_signal(
-                    ready, inc=1, device_id=at(peer_of(me, far, 0)), device_id_type=pl.DeviceIdType.MESH
-                )
-        if dz:
-            for m in range(EARLY):
-                for k in (0, 1):
-                    send_row(m, dz, k)
-
-    pl.semaphore_wait(ready, len(DZ_ORDER) - 1)
-    for m in range(OWNED):
-        for dz in DZ_ORDER:
-            send_rows(m, dz, 1 if dz == 0 else 2 if m < EARLY else 0)
+    def meet(round_):
+        for dz in (1, 7):
+            signal(ready.at[round_], dz, 0)
+
+    def met(round_):
+        pl.semaphore_wait(ready.at[round_], 2)
+
+    momentum_of(0)
+    momentum_of(1)
+    pl.semaphore_wait(barrier, len(NEAR) + COLUMNS - 1)
+    meet(0)
+    for m in range(OWNED):
+        for dz in (1, 7):
+            for k in FIRST:
+                send_row(m, dz, k)
+    for i in range(2, 8):
+        momentum_of(i)
+    met(0)
+    meet(1)
+    for m in range(OWNED):
+        for dz in (1, 7):
+            send_rows(m, dz, len(FIRST))
+    met(1)
+    meet(2)
+    for m in range(W2):
+        for dz in (2, 6):
+            send_rows(m, dz, 0)
+    met(2)
+    meet(3)
+    for m in range(W3):
+        for dz in (3, 5):
+            send_rows(m, dz, 0)
+    met(3)
+    for m in range(OWNED):
+        for dz in (4, 3, 5, 2, 6, 0):
+            if (dz in (3, 5) and m < W3) or (dz in (2, 6) and m < W2):
+                continue
+            send_rows(m, dz, 1 if dz == 0 else 0)
     for m in range(OWNED):
         land[m, pl.ds(mine, PIECE), :] = moved_ref[me, m]
 
@@ -154,21 +190,24 @@
         power = jnp.sum(jnp.sum(whole * eye, axis=1, keepdims=True), axis=0, keepdims=True)
         scale = lax.rsqrt(power + 1e-06)
         a = whole * (scale * scale)
-        product = None
         for step in range(ITERS):
-            mixed = 3.4445 * eye - 4.775 * a + 2.0315 * dot(a, a, 1, 0)
-            product = mixed if product is None else dot(mixed, product, 1, 0)
+            rest = -4.775 * a + 2.0315 * dot(a, a, 1, 0)
             if step < ITERS - 1:
+                mixed = 3.4445 * eye + rest
                 a = dot(dot(mixed, a, 1, 0), mixed, 1, 0)
-        product = product * scale
-        for j in range(TILES // 2):
-            y = dot(product, tile_pair(m, j), 1, 0)
-            for i in (0, 1):
-                q = 2 * j + i
-                for r in (0, 1):
-                    res[m, pl.ds(2 * q + r, GROUPS, stride=PIECE), :] = y[
-                        GROUPS * r : GROUPS * (r + 1), LANES * i : LANES * (i + 1)
-                    ]
+            for j in range(TILES // 2):
+                x = tile_pair(m, j) * scale if step == 0 else mid[j]
+                y = 3.4445 * x + dot(rest, x, 1, 0)
+                if step < ITERS - 1:
+                    mid[j] = y
+                else:
+                    for i in (0, 1):
+                        q = 2 * j + i
+                        for r in (0, 1):
+                            res[m, pl.ds(2 * q + r, GROUPS, stride=PIECE), :] = y[
+                                GROUPS * r : GROUPS * (r + 1), LANES * i : LANES * (i + 1)
+                            ]
+
         def send_back(peer):
             pltpu.make_async_remote_copy(
                 src_ref=res.at[m, pl.ds(pl.multiple_of(peer * PIECE, PIECE), PIECE), :],
@@ -187,18 +226,13 @@
 
                 lax.fori_loop(1 if dz == 0 else 0, 8, one, 0)
         else:
-            for heres in Z_ORDER:
-                def one(k, _, heres=heres):
-                    for there in heres:
-                        peer = there * 8 + k
-
-                        @pl.when(peer != me)
-                        def _():
-                            send_back(peer)
-
-                    return 0
-
-                lax.fori_loop(0, 8, one, 0)
+            for cell in CELLS:
+                for peer in (2 * cell + 1, 2 * cell):
+
+                    @pl.when(peer != me)
+                    def _(peer=peer):
+                        send_back(peer)
+
         back[me, m] = res[m, pl.ds(mine, PIECE), :]
 
     gram(0)
@@ -235,7 +269,8 @@
             pltpu.VMEM((OWNED, GROUPS * PIECE, LANES), jnp.float32),
             pltpu.VMEM((OWNED, COLUMNS, SIDE, SIDE), jnp.float32),
             whole,
-            pltpu.SemaphoreType.REGULAR,
+            pltpu.VMEM((TILES // 2, SIDE, 2 * LANES), jnp.float32),
+            pltpu.SemaphoreType.REGULAR((4,)),
             pltpu.SemaphoreType.DMA((16,)),
             pltpu.SemaphoreType.DMA,
             pltpu.SemaphoreType.DMA((OWNED,)),

time: 103 us -> 103 us (level)
  the two profiles are of different devices: /device:TPU:57 before, /device:TPU:1 now
where the time goes in v4:
time: 103 us; the launch traced here: 101 us
  Pallas kernels  100 us (97%)
    pallas_call x1, Pallas kernels, update(): pl.pallas_call(kernel, out_shape=[jax.ShapeDtypeStruct(gradients.shape, j...  97.9 us

profile of v4, /device:TPU:1, one launch (start us, length us, event | category | flops | bytes accessed | tf_op | source)
XLA Modules:
  0.0 100.8 jit_solution(620664570114377551)
XLA Ops:
  0.6 97.9 %shard_map.50 = (f32[64,4,16,128]{3,2,1,0:T(8,128)S(1)}, f32[64,4,16,128]{3,2,1,0:T(8,128)S(1)}) custom-call(f32[64,4,16,128]{3,2,1,0:T(8,128)} %bitcast.25, f32[64,4,16,128]{3,2,1,0:T(8,128)} %bitcast.26, f32[64,4,16,128]{3,2,1,0:T(8,128)} %bitcast.27), custom_call_target="tpu_custom_call" | custom-call | tf_op jit(solution)/shard_map/pallas_call | solution.py:259
  98.6 2.0 %shard_map.51 = (f32[64,4,16,128]{3,2,1,0:T(8,128)}, f32[64,4,16,128]{3,2,1,0:T(8,128)}) custom-call(f32[64,4,16,128]{3,2,1,0:T(8,128)S(1)} %get-tuple-element.6.new_weight_ref, f32[64,4,16,128]{3,2,1,0:T(8,128)S(1)} %get-tuple-element.7.moved_ref), custom_call_target="tpu_custom_call" | custom-call | tf_op jit(solution)/shard_map/pallas_call | solution.py:301

commit v5 on v4

--- a/solution.py
+++ b/solution.py
@@ -291,8 +291,8 @@
         pltpu.make_async_copy(new_weight_ref, weight_out, sems.at[0]),
         pltpu.make_async_copy(moved_ref, moved_out, sems.at[1]),
     ]
-    for copy in copies:
-        copy.start()
+    for i, copy in enumerate(copies):
+        copy.start(priority=i)
     for copy in copies:
         copy.wait()
 

time: 103 us -> 103 us (level)
  no operation moved by 1% of the time
where the time goes in v5:
time: 103 us; the launch traced here: 101 us
  Pallas kernels  100 us (97%)
    pallas_call x1, Pallas kernels, update(): pl.pallas_call(kernel, out_shape=[jax.ShapeDtypeStruct(gradients.shape, j...  97.9 us

profile of v5, /device:TPU:1, one launch (start us, length us, event | category | flops | bytes accessed | tf_op | source)
XLA Modules:
  0.0 100.8 jit_solution(2833096240982203667)
XLA Ops:
  0.6 97.9 %shard_map.50 = (f32[64,4,16,128]{3,2,1,0:T(8,128)S(1)}, f32[64,4,16,128]{3,2,1,0:T(8,128)S(1)}) custom-call(f32[64,4,16,128]{3,2,1,0:T(8,128)} %bitcast.25, f32[64,4,16,128]{3,2,1,0:T(8,128)} %bitcast.26, f32[64,4,16,128]{3,2,1,0:T(8,128)} %bitcast.27), custom_call_target="tpu_custom_call" | custom-call | tf_op jit(solution)/shard_map/pallas_call | solution.py:259
  98.6 2.0 %shard_map.51 = (f32[64,4,16,128]{3,2,1,0:T(8,128)}, f32[64,4,16,128]{3,2,1,0:T(8,128)}) custom-call(f32[64,4,16,128]{3,2,1,0:T(8,128)S(1)} %get-tuple-element.6.new_weight_ref, f32[64,4,16,128]{3,2,1,0:T(8,128)S(1)} %get-tuple-element.7.moved_ref), custom_call_target="tpu_custom_call" | custom-call | tf_op jit(solution)/shard_map/pallas_call | solution.py:301
